TPU v7x, 32 devices: a whole 2x2x4 slice. The times are simulated.
32 devices in a mesh: trial: 4 (over x, core), north: 2 (over y), east: 4 (over z).
Axes of the slice: x: 2, y: 2, z: 4, core: 2. Of those that a mesh axis runs over, the one named last changes fastest.
Arguments:
- pair_state: bfloat16 [192, 48, 128], P(('trial', 'north'), 'east'), parts along dimension 0, may hold values from -6 to 6
- in_gain: float32 [128], replicated, may hold values from 0.25 to 1.75
- left_weight: bfloat16 [512, 128], P('trial'), parts along dimension 0, may hold values from -0.5 to 0.5
- right_weight: bfloat16 [512, 128], P('trial'), parts along dimension 0, may hold values from -0.5 to 0.5
- left_gate: bfloat16 [512, 128], P('trial'), parts along dimension 0, may hold values from -0.5 to 0.5
- right_gate: bfloat16 [512, 128], P('trial'), parts along dimension 0, may hold values from -0.5 to 0.5
- mid_gain: float32 [128], replicated, may hold values from 0.25 to 1.75
- out_weight: bfloat16 [512, 128], P('trial'), parts along dimension 0, may hold values from -0.5 to 0.5
- out_gate: bfloat16 [512, 128], P('trial'), parts along dimension 0, may hold values from -0.5 to 0.5
Outputs:
- triangle_out: bfloat16 [192, 48, 128], P(('trial', 'north'), 'east'), parts along dimension 0
There are 4 independent parts, one for each index of `trial`. A program takes and returns all parts, laid end to end along the dimension named above; an argument that names none is the same for every part. Nothing has to cross between parts.
All inputs are finite; a program needn't handle non-finite values.
Results may differ from a plain program's by a relative error of at most 0.015.
Values may be sent and summed in bfloat16 or wider, within the bound.
A program may use at most 64 MiB of HBM per device.

v0:
```python
import jax
import jax.numpy as jnp
from jax import lax
from jax.sharding import PartitionSpec as P


def norm_channels(values, channel_gain):
    centred = values - jnp.mean(values, axis=-1, keepdims=True)
    return (
        centred
        * lax.rsqrt(jnp.mean(centred * centred, axis=-1, keepdims=True) + 1e-05)
        * channel_gain
    )


def make_factors(pair_in, in_gain, left_weight, right_weight, left_gate, right_gate):
    ready = norm_channels(pair_in.astype(jnp.float32), in_gain).astype(jnp.bfloat16)
    ready = lax.optimization_barrier(ready)
    left = jnp.einsum("ijc,cd->ijd", ready, left_weight, preferred_element_type=jnp.float32)
    left = left * jax.nn.sigmoid(
        jnp.einsum("ijc,cd->ijd", ready, left_gate, preferred_element_type=jnp.float32)
    )
    right = jnp.einsum("ijc,cd->ijd", ready, right_weight, preferred_element_type=jnp.float32)
    right = right * jax.nn.sigmoid(
        jnp.einsum("ijc,cd->ijd", ready, right_gate, preferred_element_type=jnp.float32)
    )
    return (ready, left.astype(jnp.bfloat16), right.astype(jnp.bfloat16))


def to_pair(mixed, ready, mid_gain, out_weight, out_gate):
    scaled = norm_channels(mixed.astype(jnp.float32), mid_gain).astype(jnp.bfloat16)
    scaled = lax.optimization_barrier(scaled)
    gate = jax.nn.sigmoid(
        jnp.einsum("ijc,cd->ijd", ready, out_gate, preferred_element_type=jnp.float32)
    )
    return (
        jnp.einsum("ijd,dc->ijc", scaled, out_weight, preferred_element_type=jnp.float32) * gate
    ).astype(jnp.bfloat16)


def local(
    pair_state,
    in_gain,
    left_weight,
    right_weight,
    left_gate,
    right_gate,
    mid_gain,
    out_weight,
    out_gate,
):
    ready, left, right = make_factors(
        pair_state, in_gain, left_weight, right_weight, left_gate, right_gate
    )
    count = pair_state.shape[1] * lax.axis_size("east")
    left_lines, right_lines = (
        lax.all_to_all(left, "east", split_axis=2, concat_axis=1, tiled=True),
        lax.all_to_all(right, "east", split_axis=2, concat_axis=1, tiled=True),
    )
    strip = jnp.einsum(
        "ikd,jkd->ijd",
        left_lines,
        lax.all_gather(right_lines, "north", axis=0, tiled=True),
        preferred_element_type=jnp.float32,
    )
    strip = (strip * count ** (-0.5)).astype(jnp.bfloat16)
    mixed = lax.all_to_all(strip, "east", split_axis=1, concat_axis=2, tiled=True)
    return to_pair(mixed, ready, mid_gain, out_weight, out_gate)


def solution(mesh):
    return jax.shard_map(
        local,
        mesh=mesh,
        in_specs=(
            P(("trial", "north"), "east", None),
            P(),
            P("trial", None),
            P("trial", None),
            P("trial", None),
            P("trial", None),
            P(),
            P("trial", None),
            P("trial", None),
        ),
        out_specs=P(("trial", "north"), "east", None),
        check_vma=False,
    )
```

profile of v0, /device:TPU:0, one launch (start us, length us, event | category | flops | bytes accessed | tf_op | source)
XLA Modules:
  0.0 44.6 jit_solution(821063206014544712)
XLA Ops:
  0.0 0.0 copy-start
  0.0 0.0 copy-start.1
  0.0 1.1 %convert_reduce_fusion = f32[24,12]{0,1:T(8,128)S(1)} fusion(bf16[24,12,128]{2,0,1:T(8,128)(2,1)} %param.9), kind=kLoop, calls=%fused_computation.25 | loop fusion | flops 73440 | bytes 74880 | tf_op jit(solution)/shard_map/reduce_sum | solution.py:8
  1.1 0.0 copy-done.1
  1.1 0.2 fusion.20
  1.3 0.0 copy-start.4
  1.3 0.6 %copy-done.4 = f32[128]{0:T(128)S(1)} copy-done((f32[128]{0:T(128)S(1)}, f32[128]{0:T(128)}, u32[]{:S(2)}) %copy-start.4) | copy-done | bytes 536
  2.0 0.1 fusion.22
  2.1 0.0 copy-done
  2.1 0.0 copy-start.6
  2.1 0.2 fusion.30
  2.3 0.6 %copy-done.6 = bf16[128,128]{1,0:T(8,128)(2,1)S(1)} copy-done((bf16[128,128]{1,0:T(8,128)(2,1)S(1)}, bf16[128,128]{1,0:T(8,128)(2,1)}, u32[]{:S(2)}) %copy-start.6) | copy-done | bytes 32792
  2.9 0.2 fusion.16
  3.1 0.4 copy.34
  3.5 1.1 %reshape.41 = bf16[4,2,4608]{2,1,0:T(2,128)(2,1)} reshape(bf16[128,12,24]{2,1,0:T(8,128)(2,1)S(1)} %bitcast.55) | data formatting | bytes 147456
  4.7 0.0 copy-start.2
  4.7 6.5 %all-to-all-start = ((bf16[4,2,4608]{2,1,0:T(2,128)(2,1)}), bf16[4,2,4608]{2,1,0:T(2,128)(2,1)S(1)}, u32[]{:S(2)}, u32[]{:S(2)}) async-start(bf16[4,2,4608]{2,1,0:T(2,128)(2,1)} %reshape.41), calls=%async_computation | async-start | bytes 147456 | tf_op jit(solution)/shard_map/all_to_all | solution.py:58
  11.1 0.0 copy-done.2
  11.1 0.0 copy-start.7
  11.1 0.2 fusion.27
  11.3 0.6 %copy-done.7 = bf16[128,128]{1,0:T(8,128)(2,1)S(1)} copy-done((bf16[128,128]{1,0:T(8,128)(2,1)S(1)}, bf16[128,128]{1,0:T(8,128)(2,1)}, u32[]{:S(2)}) %copy-start.7) | copy-done | bytes 32792
  11.9 0.2 fusion.15
  12.1 0.4 copy.37
  12.5 1.1 %reshape.43 = bf16[4,2,4608]{2,1,0:T(2,128)(2,1)} reshape(bf16[128,12,24]{2,1,0:T(8,128)(2,1)S(1)} %bitcast.56) | data formatting | bytes 147456
  13.7 3.2 %all-to-all-done = bf16[4,2,4608]{2,1,0:T(2,128)(2,1)S(1)} async-done(((bf16[4,2,4608]{2,1,0:T(2,128)(2,1)}), bf16[4,2,4608]{2,1,0:T(2,128)(2,1)S(1)}, u32[]{:S(2)}, u32[]{:S(2)}) %all-to-all-start) | async-done | bytes 73760 | tf_op jit(solution)/shard_map/all_to_all | solution.py:58
  16.9 3.3 %all-to-all-start.1 = ((bf16[4,2,4608]{2,1,0:T(2,128)(2,1)}), bf16[4,2,4608]{2,1,0:T(2,128)(2,1)S(1)}, u32[]{:S(2)}, u32[]{:S(2)}) async-start(bf16[4,2,4608]{2,1,0:T(2,128)(2,1)} %reshape.43), calls=%async_computation.1 | async-start | bytes 147456 | tf_op jit(solution)/shard_map/all_to_all | solution.py:57
  20.2 0.6 %reshape.42 = bf16[128,12,24]{2,1,0:T(8,128)(2,1)S(1)} reshape(bf16[4,2,4608]{2,1,0:T(2,128)(2,1)S(1)} %all-to-all-done) | data formatting | bytes 147456
  20.8 0.4 copy.35
  21.2 0.3 copy.36
  21.5 6.3 %all_gather.3 = bf16[48,48,32]{1,0,2:T(8,128)(2,1)S(1)} all-gather(bf16[24,48,32]{1,0,2:T(8,128)(2,1)S(1)} %copy.36), channel_id=1, replica_groups=mesh['trial'=4,'north'=2,'east'=4] {'north'}, dimensions={0}, use_global_device_ids=true | all-gather | bytes 221184 | tf_op jit(solution)/shard_map/all_gather | solution.py:63
  27.8 0.0 all-to-all-done.1
  27.8 0.6 %reshape.44 = bf16[128,12,24]{2,1,0:T(8,128)(2,1)S(1)} reshape(bf16[4,2,4608]{2,1,0:T(2,128)(2,1)S(1)} %all-to-all-done.1) | data formatting | bytes 147456
  28.4 0.4 copy.38
  28.8 0.3 copy.39
  29.1 0.3 fusion.1
  29.4 0.2 copy.40
  29.6 0.3 reshape.45
  29.9 10.6 %all_to_all.45 = bf16[4,2,4608]{2,1,0:T(2,128)(2,1)S(1)} all-to-all(bf16[4,2,4608]{2,1,0:T(2,128)(2,1)S(1)} %reshape.45), channel_id=1, replica_groups=mesh['trial'=4,'north'=2,'east'=4] {'east'}, dimensions={0} | all-to-all | bytes 147456 | tf_op jit(solution)/shard_map/all_to_all | solution.py:67
  40.5 0.2 reshape.46
  40.7 0.1 fusion.17
  40.9 0.2 multiply_reduce_fusion
  41.2 0.4 copy.41
  41.6 0.0 copy-start.5
  41.6 0.3 reshape.32
  41.9 0.4 copy-done.5
  42.2 0.0 copy-start.3
  42.2 0.1 multiply_convert_fusion
  42.4 0.6 %copy-done.3 = bf16[128,128]{1,0:T(8,128)(2,1)S(1)} copy-done((bf16[128,128]{1,0:T(8,128)(2,1)S(1)}, bf16[128,128]{1,0:T(8,128)(2,1)}, u32[]{:S(2)}) %copy-start.3) | copy-done | bytes 32792
  43.0 0.0 copy-start.8
  43.0 0.2 fusion.24
  43.2 0.6 %copy-done.8 = bf16[128,128]{1,0:T(8,128)(2,1)S(1)} copy-done((bf16[128,128]{1,0:T(8,128)(2,1)S(1)}, bf16[128,128]{1,0:T(8,128)(2,1)}, u32[]{:S(2)}) %copy-start.8) | copy-done | bytes 32792
  43.7 0.8 %fusion.14 = bf16[24,12,128]{2,0,1:T(8,128)(2,1)} fusion(f32[24,12,128]{2,0,1:T(8,128)S(1)} %fusion.24, bf16[24,12,128]{2,0,1:T(8,128)(2,1)S(1)} %fusion.22, bf16[128,128]{1,0:T(8,128)(2,1)S(1)} %copy-done.8), kind=kOutput, calls=%fused_computation.18 | convolution fusion | flops 9621504 | bytes 327680 | tf_op jit(solution)/shard_map/ijc,cd->ijd/dot_general | solution.py:34
  (5 shorter events, 0.1 us)
Async XLA Ops:
  0.0 2.1 %copy-start = (bf16[128,128]{1,0:T(8,128)(2,1)S(1)}, bf16[128,128]{1,0:T(8,128)(2,1)}, u32[]{:S(2)}) copy-start(bf16[128,128]{1,0:T(8,128)(2,1)} %param.12) | copy-start | bytes 98308
  0.0 1.1 %copy-start.1 = (bf16[24,12,128]{2,0,1:T(8,128)(2,1)S(1)}, bf16[24,12,128]{2,0,1:T(8,128)(2,1)}, u32[]{:S(2)}) copy-start(bf16[24,12,128]{2,0,1:T(8,128)(2,1)} %param.9) | copy-start | bytes 221188
  1.3 0.7 %copy-start.4 = (f32[128]{0:T(128)S(1)}, f32[128]{0:T(128)}, u32[]{:S(2)}) copy-start(f32[128]{0:T(128)} %param.10) | copy-start | bytes 1540
  2.1 0.8 %copy-start.6 = (bf16[128,128]{1,0:T(8,128)(2,1)S(1)}, bf16[128,128]{1,0:T(8,128)(2,1)}, u32[]{:S(2)}) copy-start(bf16[128,128]{1,0:T(8,128)(2,1)} %param.14) | copy-start | bytes 98308
  4.7 6.5 %copy-start.2 = (bf16[128,128]{1,0:T(8,128)(2,1)S(1)}, bf16[128,128]{1,0:T(8,128)(2,1)}, u32[]{:S(2)}) copy-start(bf16[128,128]{1,0:T(8,128)(2,1)} %param.11) | copy-start | bytes 98308
  4.7 12.2 %all-to-all-start = ((bf16[4,2,4608]{2,1,0:T(2,128)(2,1)}), bf16[4,2,4608]{2,1,0:T(2,128)(2,1)S(1)}, u32[]{:S(2)}, u32[]{:S(2)}) async-start(bf16[4,2,4608]{2,1,0:T(2,128)(2,1)} %reshape.41), calls=%async_computation | async-start | bytes 147456 | tf_op jit(solution)/shard_map/all_to_all | solution.py:58
  11.1 0.8 %copy-start.7 = (bf16[128,128]{1,0:T(8,128)(2,1)S(1)}, bf16[128,128]{1,0:T(8,128)(2,1)}, u32[]{:S(2)}) copy-start(bf16[128,128]{1,0:T(8,128)(2,1)} %param.13) | copy-start | bytes 98308
  16.9 10.9 %all-to-all-start.1 = ((bf16[4,2,4608]{2,1,0:T(2,128)(2,1)}), bf16[4,2,4608]{2,1,0:T(2,128)(2,1)S(1)}, u32[]{:S(2)}, u32[]{:S(2)}) async-start(bf16[4,2,4608]{2,1,0:T(2,128)(2,1)} %reshape.43), calls=%async_computation.1 | async-start | bytes 147456 | tf_op jit(solution)/shard_map/all_to_all | solution.py:57
  41.6 0.7 %copy-start.5 = (f32[128]{0:T(128)S(1)}, f32[128]{0:T(128)}, u32[]{:S(2)}) copy-start(f32[128]{0:T(128)} %param.15) | copy-start | bytes 1540
  42.2 0.8 %copy-start.3 = (bf16[128,128]{1,0:T(8,128)(2,1)S(1)}, bf16[128,128]{1,0:T(8,128)(2,1)}, u32[]{:S(2)}) copy-start(bf16[128,128]{1,0:T(8,128)(2,1)} %param.16) | copy-start | bytes 98308
  43.0 0.8 %copy-start.8 = (bf16[128,128]{1,0:T(8,128)(2,1)S(1)}, bf16[128,128]{1,0:T(8,128)(2,1)}, u32[]{:S(2)}) copy-start(bf16[128,128]{1,0:T(8,128)(2,1)} %param.17) | copy-start | bytes 98308
where the time goes:
time: 45.3 us; the launch traced here: 44.6 us
  blocking collectives  17 us (38%)
  local copies, waits for them, and re-layouts  10.4 us (23%)
  starting transfers between devices  9.77 us (22%)
  waiting for transfers between devices  3.24 us (7%)
  matrix products  2.02 us (4%)
  other arithmetic  1.96 us (4%)
    all_to_all x1, blocking collectives, local(): lax.all_to_all(strip, 'east', split_axis=1, concat_axis=2, tiled=True)  10.6 us
    unnamed x24, local copies, waits for them, and re-layouts  7.31 us
    all_to_all x1, starting transfers between devices, local(): lax.all_to_all(right, 'east', split_axis=2, concat_axis=1, tiled=True)  6.48 us
    all_gather x1, blocking collectives, local(): lax.all_gather(right_lines, 'north', axis=0, tiled=True)  6.34 us
    all_to_all x1, starting transfers between devices, local(): lax.all_to_all(left, 'east', split_axis=2, concat_axis=1, tiled=True)  3.29 us
    all_to_all x1, waiting for transfers between devices, local(): lax.all_to_all(right, 'east', split_axis=2, concat_axis=1, tiled=True)  3.23 us
    reduce_sum x2, other arithmetic, norm_channels(): centred = values - jnp.mean(values, axis=-1, keepdims=True)  1.19 us
  transfers between devices with their start and end apart: 2, of which 1 were waited for; matrix products, arithmetic and copies ran while one was open for 7% of the time, Pallas kernels for 0%

commit v1 on v0

--- a/solution.py
+++ b/solution.py
@@ -64,7 +64,12 @@
         preferred_element_type=jnp.float32,
     )
     strip = (strip * count ** (-0.5)).astype(jnp.bfloat16)
-    mixed = lax.all_to_all(strip, "east", split_axis=1, concat_axis=2, tiled=True)
+    raw_out = lax.axis_size("east")
+    wide_out = jnp.split(strip, raw_out, axis=1)
+    mixed = jnp.concatenate(
+        lax.all_to_all(jnp.stack(wide_out, axis=0), concat_axis=0, axis_name="east", split_axis=0),
+        axis=2,
+    )
     return to_pair(mixed, ready, mid_gain, out_weight, out_gate)
 
 

time: 45.3 us -> 46.4 us (1.024)
  local copies, waits for them, and re-layouts: 10.4 us -> 11.4 us
    another operation x0 -> x5, local copies, waits for them, and re-layouts: none -> 1.27 us  [local(): jnp.stack(wide_out, axis=0)]
where the time goes in v1:
time: 46.4 us; the launch traced here: 45.7 us
  blocking collectives  17 us (37%)
  local copies, waits for them, and re-layouts  11.4 us (25%)
  starting transfers between devices  9.77 us (21%)
  waiting for transfers between devices  3.24 us (7%)
  other arithmetic  2.04 us (4%)
  matrix products  2.02 us (4%)
    all_to_all x1, blocking collectives, local(): lax.all_to_all(jnp.stack(wide_out, axis=0), concat_axis=0, axis_name='eas...  10.6 us
    unnamed x24, local copies, waits for them, and re-layouts  7.32 us
    all_to_all x1, starting transfers between devices, local(): lax.all_to_all(right, 'east', split_axis=2, concat_axis=1, tiled=True)  6.48 us
    all_gather x1, blocking collectives, local(): lax.all_gather(right_lines, 'north', axis=0, tiled=True)  6.34 us
    all_to_all x1, starting transfers between devices, local(): lax.all_to_all(left, 'east', split_axis=2, concat_axis=1, tiled=True)  3.29 us
    all_to_all x1, waiting for transfers between devices, local(): lax.all_to_all(right, 'east', split_axis=2, concat_axis=1, tiled=True)  3.23 us
    another operation x5, local copies, waits for them, and re-layouts, local(): jnp.stack(wide_out, axis=0)  1.27 us
    reduce_sum x2, other arithmetic, norm_channels(): centred = values - jnp.mean(values, axis=-1, keepdims=True)  1.19 us
  transfers between devices with their start and end apart: 2, of which 1 were waited for; matrix products, arithmetic and copies ran while one was open for 7% of the time, Pallas kernels for 0%

profile of v1, /device:TPU:0, one launch (start us, length us, event | category | flops | bytes accessed | tf_op | source)
XLA Modules:
  0.0 45.7 jit_solution(8479987753498319219)
XLA Ops:
  0.0 0.0 copy-start
  0.0 0.0 copy-start.1
  0.0 1.1 %convert_reduce_fusion = f32[24,12]{0,1:T(8,128)S(1)} fusion(bf16[24,12,128]{2,0,1:T(8,128)(2,1)} %param.9), kind=kLoop, calls=%fused_computation.30 | loop fusion | flops 73440 | bytes 74880 | tf_op jit(solution)/shard_map/reduce_sum | solution.py:8
  1.1 0.0 copy-done.1
  1.1 0.2 fusion.20
  1.3 0.0 copy-start.4
  1.3 0.6 %copy-done.4 = f32[128]{0:T(128)S(1)} copy-done((f32[128]{0:T(128)S(1)}, f32[128]{0:T(128)}, u32[]{:S(2)}) %copy-start.4) | copy-done | bytes 536
  2.0 0.1 fusion.22
  2.1 0.0 copy-done
  2.1 0.0 copy-start.6
  2.1 0.2 fusion.30
  2.3 0.6 %copy-done.6 = bf16[128,128]{1,0:T(8,128)(2,1)S(1)} copy-done((bf16[128,128]{1,0:T(8,128)(2,1)S(1)}, bf16[128,128]{1,0:T(8,128)(2,1)}, u32[]{:S(2)}) %copy-start.6) | copy-done | bytes 32792
  2.9 0.2 fusion.16
  3.1 0.4 copy.36
  3.5 1.1 %reshape.37 = bf16[4,2,4608]{2,1,0:T(2,128)(2,1)} reshape(bf16[128,12,24]{2,1,0:T(8,128)(2,1)S(1)} %bitcast.62) | data formatting | bytes 147456
  4.7 0.0 copy-start.2
  4.7 6.5 %all-to-all-start = ((bf16[4,2,4608]{2,1,0:T(2,128)(2,1)}), bf16[4,2,4608]{2,1,0:T(2,128)(2,1)S(1)}, u32[]{:S(2)}, u32[]{:S(2)}) async-start(bf16[4,2,4608]{2,1,0:T(2,128)(2,1)} %reshape.37), calls=%async_computation | async-start | bytes 147456 | tf_op jit(solution)/shard_map/all_to_all | solution.py:58
  11.1 0.0 copy-done.2
  11.1 0.0 copy-start.7
  11.1 0.2 fusion.27
  11.3 0.6 %copy-done.7 = bf16[128,128]{1,0:T(8,128)(2,1)S(1)} copy-done((bf16[128,128]{1,0:T(8,128)(2,1)S(1)}, bf16[128,128]{1,0:T(8,128)(2,1)}, u32[]{:S(2)}) %copy-start.7) | copy-done | bytes 32792
  11.9 0.2 fusion.15
  12.1 0.4 copy.39
  12.5 1.1 %reshape.39 = bf16[4,2,4608]{2,1,0:T(2,128)(2,1)} reshape(bf16[128,12,24]{2,1,0:T(8,128)(2,1)S(1)} %bitcast.63) | data formatting | bytes 147456
  13.7 3.2 %all-to-all-done = bf16[4,2,4608]{2,1,0:T(2,128)(2,1)S(1)} async-done(((bf16[4,2,4608]{2,1,0:T(2,128)(2,1)}), bf16[4,2,4608]{2,1,0:T(2,128)(2,1)S(1)}, u32[]{:S(2)}, u32[]{:S(2)}) %all-to-all-start) | async-done | bytes 73760 | tf_op jit(solution)/shard_map/all_to_all | solution.py:58
  16.9 3.3 %all-to-all-start.1 = ((bf16[4,2,4608]{2,1,0:T(2,128)(2,1)}), bf16[4,2,4608]{2,1,0:T(2,128)(2,1)S(1)}, u32[]{:S(2)}, u32[]{:S(2)}) async-start(bf16[4,2,4608]{2,1,0:T(2,128)(2,1)} %reshape.39), calls=%async_computation.1 | async-start | bytes 147456 | tf_op jit(solution)/shard_map/all_to_all | solution.py:57
  20.2 0.6 %reshape.38 = bf16[128,12,24]{2,1,0:T(8,128)(2,1)S(1)} reshape(bf16[4,2,4608]{2,1,0:T(2,128)(2,1)S(1)} %all-to-all-done) | data formatting | bytes 147456
  20.8 0.4 copy.37
  21.2 0.3 copy.38
  21.5 6.3 %all_gather.3 = bf16[48,48,32]{1,0,2:T(8,128)(2,1)S(1)} all-gather(bf16[24,48,32]{1,0,2:T(8,128)(2,1)S(1)} %copy.38), channel_id=1, replica_groups=mesh['trial'=4,'north'=2,'east'=4] {'north'}, dimensions={0}, use_global_device_ids=true | all-gather | bytes 221184 | tf_op jit(solution)/shard_map/all_gather | solution.py:63
  27.8 0.0 all-to-all-done.1
  27.8 0.6 %reshape.40 = bf16[128,12,24]{2,1,0:T(8,128)(2,1)S(1)} reshape(bf16[4,2,4608]{2,1,0:T(2,128)(2,1)S(1)} %all-to-all-done.1) | data formatting | bytes 147456
  28.4 0.4 copy.40
  28.8 0.3 copy.41
  29.1 0.3 fusion.1
  29.4 0.2 slice_bitcast_fusion.3
  29.6 0.3 copy.42
  29.9 0.3 copy.45
  30.1 0.3 copy.44
  30.4 0.3 copy.43
  30.7 0.1 fusion.32
  30.8 0.3 reshape.41
  31.0 10.6 %all_to_all.41 = bf16[4,2,4608]{2,1,0:T(2,128)(2,1)S(1)} all-to-all(bf16[4,2,4608]{2,1,0:T(2,128)(2,1)S(1)} %reshape.41), channel_id=1, replica_groups=mesh['trial'=4,'north'=2,'east'=4] {'east'}, dimensions={0} | all-to-all | bytes 147456 | tf_op jit(solution)/shard_map/all_to_all | solution.py:70
  41.7 0.2 reshape.42
  41.9 0.1 fusion.17
  42.1 0.2 multiply_reduce_fusion
  42.3 0.4 copy.46
  42.7 0.0 copy-start.5
  42.7 0.3 reshape.30
  43.0 0.4 copy-done.5
  43.4 0.0 copy-start.3
  43.4 0.1 multiply_convert_fusion
  43.5 0.6 %copy-done.3 = bf16[128,128]{1,0:T(8,128)(2,1)S(1)} copy-done((bf16[128,128]{1,0:T(8,128)(2,1)S(1)}, bf16[128,128]{1,0:T(8,128)(2,1)}, u32[]{:S(2)}) %copy-start.3) | copy-done | bytes 32792
  44.1 0.0 copy-start.8
  44.1 0.2 fusion.24
  44.3 0.6 %copy-done.8 = bf16[128,128]{1,0:T(8,128)(2,1)S(1)} copy-done((bf16[128,128]{1,0:T(8,128)(2,1)S(1)}, bf16[128,128]{1,0:T(8,128)(2,1)}, u32[]{:S(2)}) %copy-start.8) | copy-done | bytes 32792
  44.9 0.8 %fusion.14 = bf16[24,12,128]{2,0,1:T(8,128)(2,1)} fusion(f32[24,12,128]{2,0,1:T(8,128)S(1)} %fusion.24, bf16[24,12,128]{2,0,1:T(8,128)(2,1)S(1)} %fusion.22, bf16[128,128]{1,0:T(8,128)(2,1)S(1)} %copy-done.8), kind=kOutput, calls=%fused_computation.18 | convolution fusion | flops 9621504 | bytes 327680 | tf_op jit(solution)/shard_map/ijc,cd->ijd/dot_general | solution.py:34
  (5 shorter events, 0.1 us)
Async XLA Ops:
  0.0 2.1 %copy-start = (bf16[128,128]{1,0:T(8,128)(2,1)S(1)}, bf16[128,128]{1,0:T(8,128)(2,1)}, u32[]{:S(2)}) copy-start(bf16[128,128]{1,0:T(8,128)(2,1)} %param.12) | copy-start | bytes 98308
  0.0 1.1 %copy-start.1 = (bf16[24,12,128]{2,0,1:T(8,128)(2,1)S(1)}, bf16[24,12,128]{2,0,1:T(8,128)(2,1)}, u32[]{:S(2)}) copy-start(bf16[24,12,128]{2,0,1:T(8,128)(2,1)} %param.9) | copy-start | bytes 221188
  1.3 0.7 %copy-start.4 = (f32[128]{0:T(128)S(1)}, f32[128]{0:T(128)}, u32[]{:S(2)}) copy-start(f32[128]{0:T(128)} %param.10) | copy-start | bytes 1540
  2.1 0.8 %copy-start.6 = (bf16[128,128]{1,0:T(8,128)(2,1)S(1)}, bf16[128,128]{1,0:T(8,128)(2,1)}, u32[]{:S(2)}) copy-start(bf16[128,128]{1,0:T(8,128)(2,1)} %param.14) | copy-start | bytes 98308
  4.7 6.5 %copy-start.2 = (bf16[128,128]{1,0:T(8,128)(2,1)S(1)}, bf16[128,128]{1,0:T(8,128)(2,1)}, u32[]{:S(2)}) copy-start(bf16[128,128]{1,0:T(8,128)(2,1)} %param.11) | copy-start | bytes 98308
  4.7 12.2 %all-to-all-start = ((bf16[4,2,4608]{2,1,0:T(2,128)(2,1)}), bf16[4,2,4608]{2,1,0:T(2,128)(2,1)S(1)}, u32[]{:S(2)}, u32[]{:S(2)}) async-start(bf16[4,2,4608]{2,1,0:T(2,128)(2,1)} %reshape.37), calls=%async_computation | async-start | bytes 147456 | tf_op jit(solution)/shard_map/all_to_all | solution.py:58
  11.1 0.8 %copy-start.7 = (bf16[128,128]{1,0:T(8,128)(2,1)S(1)}, bf16[128,128]{1,0:T(8,128)(2,1)}, u32[]{:S(2)}) copy-start(bf16[128,128]{1,0:T(8,128)(2,1)} %param.13) | copy-start | bytes 98308
  16.9 10.9 %all-to-all-start.1 = ((bf16[4,2,4608]{2,1,0:T(2,128)(2,1)}), bf16[4,2,4608]{2,1,0:T(2,128)(2,1)S(1)}, u32[]{:S(2)}, u32[]{:S(2)}) async-start(bf16[4,2,4608]{2,1,0:T(2,128)(2,1)} %reshape.39), calls=%async_computation.1 | async-start | bytes 147456 | tf_op jit(solution)/shard_map/all_to_all | solution.py:57
  42.7 0.7 %copy-start.5 = (f32[128]{0:T(128)S(1)}, f32[128]{0:T(128)}, u32[]{:S(2)}) copy-start(f32[128]{0:T(128)} %param.15) | copy-start | bytes 1540
  43.4 0.8 %copy-start.3 = (bf16[128,128]{1,0:T(8,128)(2,1)S(1)}, bf16[128,128]{1,0:T(8,128)(2,1)}, u32[]{:S(2)}) copy-start(bf16[128,128]{1,0:T(8,128)(2,1)} %param.16) | copy-start | bytes 98308
  44.1 0.8 %copy-start.8 = (bf16[128,128]{1,0:T(8,128)(2,1)S(1)}, bf16[128,128]{1,0:T(8,128)(2,1)}, u32[]{:S(2)}) copy-start(bf16[128,128]{1,0:T(8,128)(2,1)} %param.17) | copy-start | bytes 98308
